TPU v7x, 32 devices: a whole 2x2x4 slice. The times are simulated.
32 devices in a mesh: grp: 4 (over y, x), dev: 8 (over z, core).
Axes of the slice: x: 2, y: 2, z: 4, core: 2. Of those that a mesh axis runs over, the one named last changes fastest.
Arguments:
- obs_coord: float32 [3, 131072], P(None, ('grp', 'dev')), may hold values from -1 to 1
- obs_resid: float32 [131072], P(('grp', 'dev')), may hold values from -6 to 6
- obs_weight: float32 [131072], P(('grp', 'dev')), may hold values from 0.5 to 2
- obs_dest: int32 [131072], P(('grp', 'dev')), may hold values from 0 to 7, as said below
- obs_send_slot: int32 [131072], P(('grp', 'dev')), may hold values from 0 to 1023, as said below
- obs_elem: int32 [131072], P(('grp', 'dev')), may hold values from 0 to 255, as said below
- obs_slot: int32 [131072], P(('grp', 'dev')), may hold values from 0 to 31, as said below
Outputs:
- nodal: float32 [16, 64, 8, 512], P('grp', 'dev')
- total_cost: float32 [], replicated
Inputs may be any that keep to these rules, and one draw needn't show every extreme that they name: `obs_dest`: from the rows of one device, at most 1024 observations go to any one destination; in every group one destination receives exactly 1024 from every device of the group. `obs_send_slot`: distinct among the rows of one device with the same obs_dest. `obs_elem`: together with obs_slot distinct among all observations of a group with the same obs_dest. `obs_slot`: on every destination some element uses all 32 slots.
All inputs are finite; a program needn't handle non-finite values.
Results may differ from a plain program's by a relative error of at most 0.00017.
Values sent between devices are 32-bit elements; how exact they have to be, the bound alone decides.
No kernel may reach another device: no remote copies, remote signals or barrier semaphores. Data moves between devices by JAX's collectives and lax.ppermute only.
A program may use at most 64 MiB of HBM per device.

v0:
```python
import math

import jax
import jax.numpy as jnp
from jax import lax
from jax.sharding import PartitionSpec as P

EX = 4
EY = 8
EZ = 8
ELEM_DEV = 256
SLOTS = 32


def with_halo(block, sides, width):
    for axis, dim in sides:
        count = lax.axis_size(axis)
        forward = [(i, i + 1) for i in range(count - 1)]
        backward = [(target, source) for source, target in forward]
        low = lax.ppermute(
            lax.slice_in_dim(block, block.shape[dim] - width, None, axis=dim), axis, forward
        )
        high = lax.ppermute(lax.slice_in_dim(block, 0, width, axis=dim), axis, backward)
        block = jnp.concatenate([low, block, high], axis=dim)
    return block


def basis_values(position):
    anchors = [-math.cos(math.pi * k / 7) for k in range(8)]
    basis = []
    for node_i in range(8):
        factor = jnp.ones_like(position)
        for node_m in range(8):
            if node_m != node_i:
                factor = factor * (
                    (position - anchors[node_m]) / (anchors[node_i] - anchors[node_m])
                )
        basis.append(factor)
    return jnp.stack(basis)


def contract(first_w, second_w, third_w):
    outer = (first_w[:, None, :] * second_w[None, :, :]).reshape(64, ELEM_DEV, SLOTS)
    third = third_w.reshape(8, ELEM_DEV, SLOTS)
    mixed = jnp.einsum("aes,kes->eak", outer, third, precision=lax.Precision.HIGHEST)
    return mixed.reshape(ELEM_DEV, 512)


def combine(field, elem_dim, node_dim, from_low, from_high):
    count = field.shape[elem_dim]
    low_plane = lax.slice_in_dim(field, 0, 1, axis=node_dim)
    high_plane = lax.slice_in_dim(field, 7, 8, axis=node_dim)
    after = jnp.concatenate(
        [lax.slice_in_dim(low_plane, 1, count, axis=elem_dim), from_high], axis=elem_dim
    )
    before = jnp.concatenate(
        [from_low, lax.slice_in_dim(high_plane, 0, count - 1, axis=elem_dim)], axis=elem_dim
    )
    middle = lax.slice_in_dim(field, 1, 7, axis=node_dim)
    return jnp.concatenate([low_plane + before, middle, high_plane + after], axis=node_dim)


def boundary(field, elem_dim, node_dim):
    count = field.shape[elem_dim]
    low_plane = lax.slice_in_dim(field, 0, 1, axis=node_dim)
    high_plane = lax.slice_in_dim(field, 7, 8, axis=node_dim)
    return jnp.concatenate(
        [
            lax.slice_in_dim(low_plane, 0, 1, axis=elem_dim),
            lax.slice_in_dim(high_plane, count - 1, count, axis=elem_dim),
        ],
        axis=elem_dim,
    )


def on_device(obs_coord, obs_resid, obs_weight, obs_dest, obs_send_slot, obs_elem, obs_slot):
    peer_count = lax.axis_size("dev")
    row_count = obs_resid.shape[0]
    capacity = 2 * row_count // peer_count
    cell_count = ELEM_DEV * SLOTS
    forcing = obs_weight * obs_resid
    total_cost = lax.psum(0.5 * jnp.sum(forcing * obs_resid), ("grp", "dev"))
    payload = jnp.concatenate([obs_coord, forcing[None, :]], axis=0)
    channels = payload.shape[0]
    target = obs_dest * capacity + obs_send_slot
    cell_ids = obs_elem * SLOTS + obs_slot
    send_values = (
        jnp.zeros((channels, peer_count * capacity), payload.dtype).at[:, target].set(payload)
    )
    send_cells = jnp.full((peer_count * capacity,), cell_count, jnp.int32).at[target].set(cell_ids)
    send_values = send_values.reshape(channels, peer_count, capacity)
    send_cells = send_cells.reshape(1, peer_count, capacity)
    got_values, got_cells = (
        lax.all_to_all(send_values, "dev", split_axis=1, concat_axis=1, tiled=True),
        lax.all_to_all(send_cells, "dev", split_axis=1, concat_axis=1, tiled=True),
    )
    packed = jnp.zeros((channels, cell_count + 1), payload.dtype)
    packed = packed.at[:, got_cells.reshape(-1)].set(got_values.reshape(channels, -1))[
        :, :cell_count
    ]
    first_w = basis_values(packed[0]) * packed[3]
    second_w = basis_values(packed[1])
    third_w = basis_values(packed[2])
    field = contract(first_w, second_w, third_w).reshape(EX, EY, EZ, 8, 8, 8)
    padded = with_halo(boundary(field, 0, 3), (("grp", 0),), 1)
    field = combine(field, 0, 3, padded[0:1], padded[3:4])
    padded = with_halo(boundary(field, 1, 4), (("dev", 1),), 1)
    field = combine(field, 1, 4, padded[:, 0:1], padded[:, 3:4])
    empty = jnp.zeros_like(lax.slice_in_dim(lax.slice_in_dim(field, 0, 1, axis=5), 0, 1, axis=2))
    field = combine(field, 2, 5, empty, empty)
    return (field.reshape(EX, EY, EZ, 512), total_cost)


def solution(mesh):
    placed = (
        P(None, ("grp", "dev")),
        P(("grp", "dev")),
        P(("grp", "dev")),
        P(("grp", "dev")),
        P(("grp", "dev")),
        P(("grp", "dev")),
        P(("grp", "dev")),
    )
    return jax.shard_map(
        on_device,
        mesh=mesh,
        in_specs=placed,
        out_specs=(P("grp", "dev", None, None), P()),
        check_vma=False,
    )
```

profile of v0, /device:TPU:1, one launch (start us, length us, event | category | flops | bytes accessed | tf_op | source)
XLA Modules:
  0.0 226.2 jit_solution(2030563538721729877)
XLA Ops:
  1.4 16.1 %scatter_custom_fusion = s32[8192]{0:T(1024)} fusion(s32[4096]{0:T(1024)S(1)} %get-tuple-element.54, s32[4096]{0:T(1024)S(1)} %get-tuple-element.55, s32[]{:T(128)} %constant.245.clone.1), kind=kCustom, calls=%fused_computation.88 | custom fusion | bytes 32772 | tf_op jit(solution)/shard_map/scatter | solution.py:90
  17.5 6.4 %all-to-all-start = ((s32[1,8,1024]{2,0,1:T(1,128)}), s32[1,8,1024]{2,0,1:T(1,128)S(1)}, u32[]{:S(2)}, u32[]{:S(2)}) async-start(s32[1,8,1024]{2,0,1:T(1,128)} %bitcast), calls=%async_computation | async-start | bytes 65536 | tf_op jit(solution)/shard_map/all_to_all | solution.py:95
  23.9 1.3 multiply_reduce_fusion.8
  26.7 39.5 %psum.7 = f32[]{:T(128)} all-reduce(f32[]{:T(128)S(6)} %mul_shard_map.3), channel_id=1, replica_groups=mesh['grp'=4,'dev'=8] {'grp','dev'}, use_global_device_ids=true, to_apply=%region_4.0 | all-reduce | flops 1 | bytes 8 | tf_op jit(solution)/shard_map/psum | solution.py:82
  66.9 12.8 %scatter_custom_fusion.1 = f32[4,8192]{0,1:T(8,128)} fusion(s32[4096]{0:T(1024)S(1)} %get-tuple-element.54, f32[4096,4]{1,0:T(8,128)S(1)} %copy.404, f32[]{:T(128)} %constant.244.clone.1), kind=kCustom, calls=%fused_computation.11 | custom fusion | bytes 131076 | tf_op jit(solution)/shard_map/scatter | solution.py:88
  79.6 3.5 %copy.405 = f32[4,8,1024]{2,0,1:T(4,128)} copy(f32[4,8,1024]{0,2,1:T(8,128)} %bitcast.26) | data formatting | bytes 262144 | tf_op jit(solution)/shard_map/reshape | solution.py:91
  83.1 4.9 %all-to-all-start.1 = ((f32[4,8,1024]{2,0,1:T(4,128)}), f32[4,8,1024]{2,0,1:T(4,128)S(1)}, u32[]{:S(2)}, u32[]{:S(2)}) async-start(f32[4,8,1024]{2,0,1:T(4,128)} %copy.405), calls=%async_computation.1 | async-start | bytes 262144 | tf_op jit(solution)/shard_map/all_to_all | solution.py:94
  88.0 5.7 %all-to-all-done.1 = f32[4,8,1024]{2,0,1:T(4,128)S(1)} async-done(((f32[4,8,1024]{2,0,1:T(4,128)}), f32[4,8,1024]{2,0,1:T(4,128)S(1)}, u32[]{:S(2)}, u32[]{:S(2)}) %all-to-all-start.1) | async-done | bytes 131104 | tf_op jit(solution)/shard_map/all_to_all | solution.py:94
  93.7 2.6 %copy.406 = f32[8192,4]{1,0:T(8,128)} copy(f32[8192,4]{0,1:T(4,128)S(1)} %bitcast.35) | data formatting | bytes 262144 | tf_op jit(solution)/shard_map/reshape | solution.py:98
  96.4 23.0 %scatter_custom_fusion.2 = f32[4,8193]{0,1:T(8,128)} fusion(s32[8192]{0:T(1024)S(1)} %bitcast.38, f32[8192,4]{1,0:T(8,128)} %copy.406, f32[]{:T(128)} %constant.244.clone.1), kind=kCustom, calls=%fused_computation.9 | custom fusion | bytes 131600 | tf_op jit(solution)/shard_map/scatter | solution.py:98
  119.4 14.8 %slice_reduce_fusion = (f32[8192]{0:T(1024)S(1)}, f32[1,8192]{0,1:T(8,128)}, f32[1,8192]{0,1:T(8,128)}, f32[1,8192]{0,1:T(8,128)}) fusion(f32[4,8193]{0,1:T(8,128)} %scatter_custom_fusion.2), kind=kLoop, calls=%fused_computation.8 | loop fusion | bytes 262144 | tf_op jit(solution)/shard_map/slice | solution.py:101
  134.2 2.8 %copy.422 = f32[1,8192]{1,0:T(1,128)S(1)} copy(f32[1,8192]{0,1:T(8,128)} %get-tuple-element.35) | data formatting | bytes 65536
  137.0 2.8 %copy.421 = f32[1,8192]{1,0:T(1,128)S(1)} copy(f32[1,8192]{0,1:T(8,128)} %get-tuple-element.36) | data formatting | bytes 65536
  139.9 2.8 %copy.423 = f32[1,8192]{1,0:T(1,128)S(1)} copy(f32[1,8192]{0,1:T(8,128)} %get-tuple-element.37) | data formatting | bytes 65536
  142.7 1.9 multiply_reduce_fusion
  149.0 4.8 %mul.732 = f32[64,256,32]{2,1,0:T(8,128)} reshape(f32[8,8,8192]{2,1,0:T(8,128)S(1)} %broadcast_multiply_fusion) | data formatting | bytes 4194304 | tf_op jit(solution)/shard_map/mul | solution.py:43
  153.8 1.6 stack.59
  155.4 20.7 %fusion = f32[256,64,8]{1,2,0:T(8,128)S(1)} fusion(f32[8,256,32]{2,0,1:T(8,128)S(1)} %stack.59, f32[64,256,32]{2,1,0:T(8,128)} %mul.732), kind=kOutput, calls=%fused_computation.6 | convolution fusion | flops 50331648 | bytes 2883584 | tf_op jit(solution)/shard_map/aes,kes->eak/dot_general | solution.py:45
  176.5 6.2 %reshape_reshape.3 = f32[4,8,8,8,8,8]{2,1,0,5,4,3:T(8,128)} reshape(f32[256,64,8]{0,2,1:T(8,128)S(1)} %copy.419) | data formatting | bytes 1048576 | tf_op jit(solution)/shard_map/reshape;reshape | solution.py:104
  183.8 3.9 %collective-permute-start = (f32[1,8,8,1,8,8]{2,1,0,5,4,3:T(8,128)S(1)}, f32[1,8,8,1,8,8]{2,1,0,5,4,3:T(8,128)S(1)}, u32[]{:S(2)}, u32[]{:S(2)}) collective-permute-start(f32[1,8,8,1,8,8]{2,1,0,5,4,3:T(8,128)S(1)} %get-tuple-element.30), channel_id=1, source_target_pairs={{0,8},{8,16},{16,24},{1,9},{9,17},{17,25},{2,10},{10,18},{18,26},{... | collective-permute-start | bytes 49160 | tf_op jit(solution)/shard_map/ppermute | solution.py:20
  187.7 1.3 collective-permute-start.1
  189.0 1.5 fusion.15
  190.5 3.5 %slice.118 = f32[4,8,8,6,8,8]{2,1,0,5,4,3:T(8,128)S(1)} slice(f32[4,8,8,8,8,8]{2,1,0,5,4,3:T(8,128)} %reshape_reshape.3), slice={[0:4], [0:8], [0:8], [1:7], [0:8], [0:8]} | slice | bytes 786432 | tf_op jit(solution)/shard_map/slice | solution.py:59
  194.0 6.1 %collective-permute-done.1 = f32[1,8,8,1,8,8]{2,1,0,5,4,3:T(8,128)S(1)} collective-permute-done((f32[1,8,8,1,8,8]{2,1,0,5,4,3:T(8,128)S(1)}, f32[1,8,8,1,8,8]{2,1,0,5,4,3:T(8,128)S(1)}, u32[]{:S(2)}, u32[]{:S(2)}) %collective-permute-start.1) | collective-permute-done | bytes 16416 | tf_op jit(solution)/shard_map/ppermute | solution.py:23
  200.1 1.9 slice_add_fusion.1
  202.3 4.4 %collective-permute-start.2 = (f32[4,1,8,8,1,8]{2,1,0,5,4,3:T(1,128)S(1)}, f32[4,1,8,8,1,8]{2,1,0,5,4,3:T(1,128)S(1)}, u32[]{:S(2)}, u32[]{:S(2)}) collective-permute-start(f32[4,1,8,8,1,8]{2,1,0,5,4,3:T(1,128)S(1)} %get-tuple-element.26), channel_id=1, source_target_pairs={{0,1},{1,2},{2,3},{3,4},{4,5},{5,6},{6,7},{8,9},{9,10},{10,11},{11... | collective-permute-start | bytes 24584 | tf_op jit(solution)/shard_map/ppermute | solution.py:20
  206.7 1.9 collective-permute-start.3
  208.6 1.9 pad_maximum_fusion
  210.5 1.2 slice.122
  214.1 1.6 pad_maximum_fusion.1
  216.6 3.7 %pad_maximum_fusion.2 = f32[4,8,8,8,8,8]{2,1,0,5,4,3:T(8,128)} fusion(f32[4,8,8,8,8,1]{2,1,0,5,4,3:T(8,128)S(1)} %get-tuple-element.23, f32[4,8,8,8,8,6]{2,1,0,5,4,3:T(8,128)S(1)} %slice.123, f32[4,8,8,8,8,1]{2,1,0,5,4,3:T(8,128)S(1)} %get-tuple-element.22), kind=kLoop, calls=%fused_computation.5 | loop fusion | flops 262144 | bytes 1048576 | tf_op jit(solution)/shard_map/concatenate | solution.py:60
  220.3 5.9 %copy.420 = f32[4,8,8,512]{3,2,1,0:T(8,128)} copy(f32[4,8,8,512]{2,1,0,3:T(8,128)} %bitcast.25) | data formatting | bytes 1048576
  (30 shorter events, 11.6 us)
Async XLA Ops:
  17.5 65.6 %all-to-all-start = ((s32[1,8,1024]{2,0,1:T(1,128)}), s32[1,8,1024]{2,0,1:T(1,128)S(1)}, u32[]{:S(2)}, u32[]{:S(2)}) async-start(s32[1,8,1024]{2,0,1:T(1,128)} %bitcast), calls=%async_computation | async-start | bytes 65536 | tf_op jit(solution)/shard_map/all_to_all | solution.py:95
  83.1 10.6 %all-to-all-start.1 = ((f32[4,8,1024]{2,0,1:T(4,128)}), f32[4,8,1024]{2,0,1:T(4,128)S(1)}, u32[]{:S(2)}, u32[]{:S(2)}) async-start(f32[4,8,1024]{2,0,1:T(4,128)} %copy.405), calls=%async_computation.1 | async-start | bytes 262144 | tf_op jit(solution)/shard_map/all_to_all | solution.py:94
  149.0 4.8 %copy-start = (f32[1,256,32]{2,1,0:T(8,128)S(1)}, f32[1,256,32]{2,1,0:T(8,128)}, u32[]{:S(2)}) copy-start(f32[1,256,32]{2,1,0:T(8,128)} %stack.24) | copy-start | bytes 98308
  183.8 10.2 %collective-permute-start = (f32[1,8,8,1,8,8]{2,1,0,5,4,3:T(8,128)S(1)}, f32[1,8,8,1,8,8]{2,1,0,5,4,3:T(8,128)S(1)}, u32[]{:S(2)}, u32[]{:S(2)}) collective-permute-start(f32[1,8,8,1,8,8]{2,1,0,5,4,3:T(8,128)S(1)} %get-tuple-element.30), channel_id=1, source_target_pairs={{0,8},{8,16},{16,24},{1,9},{9,17},{17,25},{2,10},{10,18},{18,26},{... | collective-permute-start | bytes 49160 | tf_op jit(solution)/shard_map/ppermute | solution.py:20
  187.7 12.4 %collective-permute-start.1 = (f32[1,8,8,1,8,8]{2,1,0,5,4,3:T(8,128)S(1)}, f32[1,8,8,1,8,8]{2,1,0,5,4,3:T(8,128)S(1)}, u32[]{:S(2)}, u32[]{:S(2)}) collective-permute-start(f32[1,8,8,1,8,8]{2,1,0,5,4,3:T(8,128)S(1)} %get-tuple-element.31), channel_id=1, source_target_pairs={{8,0},{16,8},{24,16},{9,1},{17,9},{25,17},{10,2},{18,10},{26,18},{... | collective-permute-start | bytes 49160 | tf_op jit(solution)/shard_map/ppermute | solution.py:23
  202.3 9.4 %collective-permute-start.2 = (f32[4,1,8,8,1,8]{2,1,0,5,4,3:T(1,128)S(1)}, f32[4,1,8,8,1,8]{2,1,0,5,4,3:T(1,128)S(1)}, u32[]{:S(2)}, u32[]{:S(2)}) collective-permute-start(f32[4,1,8,8,1,8]{2,1,0,5,4,3:T(1,128)S(1)} %get-tuple-element.26), channel_id=1, source_target_pairs={{0,1},{1,2},{2,3},{3,4},{4,5},{5,6},{6,7},{8,9},{9,10},{10,11},{11... | collective-permute-start | bytes 24584 | tf_op jit(solution)/shard_map/ppermute | solution.py:20
  206.7 6.3 %collective-permute-start.3 = (f32[4,1,8,8,1,8]{2,1,0,5,4,3:T(1,128)S(1)}, f32[4,1,8,8,1,8]{2,1,0,5,4,3:T(1,128)S(1)}, u32[]{:S(2)}, u32[]{:S(2)}) collective-permute-start(f32[4,1,8,8,1,8]{2,1,0,5,4,3:T(1,128)S(1)} %get-tuple-element.27), channel_id=1, source_target_pairs={{1,0},{2,1},{3,2},{4,3},{5,4},{6,5},{7,6},{9,8},{10,9},{11,10},{12... | collective-permute-start | bytes 24584 | tf_op jit(solution)/shard_map/ppermute | solution.py:23
where the time goes:
time: 227 us; the launch traced here: 226 us
  local copies, waits for them, and re-layouts  111 us (49%)
  blocking collectives  39.5 us (17%)
  starting transfers between devices  22.7 us (10%)
  matrix products  20.7 us (9%)
  other arithmetic  17.6 us (8%)
  waiting for transfers between devices  13 us (6%)
    psum x1, blocking collectives, on_device(): total_cost = lax.psum(0.5 * jnp.sum(forcing * obs_resid), ('grp', 'dev'))  39.5 us
    scatter x1, local copies, waits for them, and re-layouts, on_device(): packed.at[:, got_cells.reshape(-1)].set(got_values.reshape(channels, -1))  23 us
    dot_general x1, matrix products, contract(): jnp.einsum('aes,kes->eak', outer, third, precision=lax.Precision.HIGHEST)  20.7 us
    scatter x1, local copies, waits for them, and re-layouts, on_device(): jnp.full((peer_count * capacity,), cell_count, jnp.int32).at[target]  16.1 us
    slice x1, local copies, waits for them, and re-layouts, on_device(): first_w = basis_values(packed[0]) * packed[3]  14.8 us
    unnamed x6, local copies, waits for them, and re-layouts  14.4 us
    scatter x1, local copies, waits for them, and re-layouts, on_device(): jnp.zeros((channels, peer_count * capacity), payload.dtype).at[:, target]  12.8 us
    ppermute x2, starting transfers between devices, with_halo(): lax.ppermute(lax.slice_in_dim(block, block.shape[dim] - width, None, axis...  8.28 us
  transfers between devices with their start and end apart: 6, of which 3 were waited for; matrix products, arithmetic and copies ran while one was open for 12% of the time, Pallas kernels for 0%

commit v1 on v0

v1 whole, which is shorter than its diff:
```python
import functools
import math

import jax
import jax.numpy as jnp
from jax import lax
from jax.experimental import pallas as pl
from jax.experimental.pallas import tpu as pltpu
from jax.sharding import PartitionSpec as P

EX = 4
EY = 8
EZ = 8
ELEM_DEV = 256
NODES = 8
FIELDS = 5
ANCHORS = [-math.cos(math.pi * k / 7) for k in range(NODES)]
SCALES = [
    1.0 / math.prod(ANCHORS[i] - ANCHORS[m] for m in range(NODES) if m != i) for i in range(NODES)
]
NT = (((1,), (1,)), ((), ()))


def pieces_of(values):
    first = values.astype(jnp.bfloat16)
    rest = values - first.astype(jnp.float32)
    second = rest.astype(jnp.bfloat16)
    third = rest - second.astype(jnp.float32)
    return [first.astype(jnp.float32), second.astype(jnp.float32), third]


def pack_kernel(coord, resid, weight, dest, slot, elem, out, acc, *, capacity, wide, chunk):
    rows = resid.shape[1]
    per_peer = capacity // wide
    high_count = 2 * rows // wide
    acc[...] = jnp.zeros_like(acc)
    lane_ids = lax.broadcasted_iota(jnp.int32, (wide, chunk), 0)

    def step(i, cost):
        at = pl.ds(pl.multiple_of(i * chunk, chunk), chunk)
        residual = resid[:, at]
        forcing = weight[:, at] * residual
        target = dest[:, at] * capacity + slot[:, at]
        high = target // wide
        low = target - high * wide
        right = jnp.where(lane_ids == low, 1.0, 0.0).astype(jnp.bfloat16)
        values = jnp.concatenate(
            [
                coord[:, at],
                forcing,
                elem[:, at].astype(jnp.float32),
                jnp.zeros((8 - FIELDS, chunk), jnp.float32),
            ],
            axis=0,
        )
        high_rep = jnp.broadcast_to(high, (8, chunk))
        pieces = pieces_of(values)
        total = None
        for piece in pieces:
            left = jnp.concatenate(
                [jnp.where(high_rep == h, piece, 0.0) for h in range(high_count)], axis=0
            ).astype(jnp.bfloat16)
            part = lax.dot_general(left, right, NT, preferred_element_type=jnp.float32)
            total = part if total is None else total + part
        acc[...] += total
        return cost + forcing * residual

    cost = lax.fori_loop(0, rows // chunk, step, jnp.zeros((1, chunk), jnp.float32))
    cost = 0.5 * jnp.sum(cost, axis=1, keepdims=True)
    used = FIELDS * per_peer
    for peer in range(out.shape[0]):
        for j in range(per_peer):
            source = (peer * per_peer + j) * 8
            out[peer, FIELDS * j : FIELDS * (j + 1), :] = acc[source : source + FIELDS, :]
        out[peer, used:, :] = jnp.broadcast_to(cost, (out.shape[1] - used, wide))


def basis_of(position, node, scale):
    factor = scale
    for m in range(NODES):
        factor = factor * jnp.where(node == m, 1.0, position - ANCHORS[m])
    return factor


def field_kernel(got, field, planes, acc, elems, first, second, *, capacity, wide, block):
    peer_count = got.shape[0]
    per_peer = capacity // wide
    parts = block // wide
    node = lax.broadcasted_iota(jnp.int32, (NODES, wide), 0)
    scale = jnp.zeros((NODES, wide), jnp.float32)
    for i in range(NODES):
        scale = jnp.where(node == i, SCALES[i], scale)
    elem_ids = lax.broadcasted_iota(jnp.int32, (ELEM_DEV, wide), 0).astype(jnp.float32)
    acc[...] = jnp.zeros_like(acc)

    def step(i, carry):
        for q in range(parts):
            peer = i * (parts // per_peer) + q // per_peer
            row = FIELDS * (q % per_peer)
            u, v, w, f, e = (got[peer, row + k : row + k + 1, :] for k in range(FIELDS))
            lanes = slice(q * wide, (q + 1) * wide)
            elems[:, lanes] = jnp.where(elem_ids == e, 1.0, 0.0).astype(jnp.bfloat16)
            first_w = basis_of(u, node, scale) * f
            second_w = basis_of(v, node, scale)
            third_w = basis_of(w, node, scale)
            inner = [second_w[b : b + 1, :] * third_w for b in range(NODES)]
            for a in range(NODES):
                mine = jnp.broadcast_to(first_w[a : a + 1, :], (NODES, wide))
                whole = jnp.concatenate([mine * inner[b] for b in range(NODES)], axis=0)
                head = whole.astype(jnp.bfloat16)
                at = slice(64 * a, 64 * (a + 1))
                first[at, lanes] = head
                second[at, lanes] = (whole - head.astype(jnp.float32)).astype(jnp.bfloat16)
        chosen = elems[...]
        acc[...] += lax.dot_general(
            chosen, first[...], NT, preferred_element_type=jnp.float32
        ) + lax.dot_general(chosen, second[...], NT, preferred_element_type=jnp.float32)
        return carry

    lax.fori_loop(0, peer_count * capacity // block, step, 0)

    lane = lax.broadcasted_iota(jnp.int32, (EZ, 128), 1)
    level = lax.broadcasted_iota(jnp.int32, (EZ, 128), 0)
    take_up = jnp.logical_and(lane % 8 == 7, level < EZ - 1)
    take_down = jnp.logical_and(lane % 8 == 0, level > 0)
    columns = []
    for j in range(4):
        blocks = []
        for r in range(EX * EY):
            x = acc[8 * r : 8 * (r + 1), 128 * j : 128 * (j + 1)]
            up = pltpu.roll(pltpu.roll(x, EZ - 1, 0), 7, 1)
            down = pltpu.roll(pltpu.roll(x, 1, 0), 121, 1)
            blocks.append(x + jnp.where(take_up, up, 0.0) + jnp.where(take_down, down, 0.0))
        column = []
        for r in range(EX * EY):
            x = blocks[r]
            if r % EY < EY - 1:
                x = x + jnp.where(lane % 64 >= 56, pltpu.roll(blocks[r + 1], 56, 1), 0.0)
            if r % EY > 0:
                x = x + jnp.where(lane % 64 < 8, pltpu.roll(blocks[r - 1], 72, 1), 0.0)
            column.append(x)
        if j in (1, 2):
            for r in range(EX * EY):
                field[8 * r : 8 * (r + 1), 128 * j : 128 * (j + 1)] = column[r]
        columns.append(column)
    lower, upper = columns[0], columns[3]
    for r in range(EX * EY):
        x, y = lower[r], upper[r]
        if r >= EY:
            x = x + jnp.where(lane < 64, pltpu.roll(upper[r - EY], 64, 1), 0.0)
        if r < (EX - 1) * EY:
            y = y + jnp.where(lane >= 64, pltpu.roll(lower[r + EY], 64, 1), 0.0)
        field[8 * r : 8 * (r + 1), 0:128] = x
        field[8 * r : 8 * (r + 1), 384:512] = y
    half = EY // 2
    mine = lax.axis_index("grp")
    used = FIELDS * per_peer
    cost = got[0, used : used + 1, 0:128]
    for peer in range(1, peer_count):
        cost = cost + got[peer, used : used + 1, 0:128]
    last = (EX - 1) * EY
    for r in range(half):
        low_pack = jnp.where(lane < 64, lower[r], pltpu.roll(lower[r + half], 64, 1))
        high_pack = jnp.where(
            lane < 64, pltpu.roll(upper[last + r], 64, 1), upper[last + r + half]
        )
        for other in range(planes.shape[0]):
            message = jnp.where(other == mine - 1, low_pack, 0.0)
            planes[other, 8 * r : 8 * (r + 1), :] = jnp.where(other == mine + 1, high_pack, message)
    for other in range(planes.shape[0]):
        planes[other, 8 * half :, :] = jnp.broadcast_to(cost, (8, 128))


def neighbours(planes, lane, r):
    count = planes.shape[0]
    half = EY // 2
    mine = lax.axis_index("grp")
    below = jnp.maximum(mine - 1, 0)
    above = jnp.minimum(mine + 1, count - 1)
    at = 8 * (r % half)
    low = planes[below, at : at + 8, :]
    high = planes[above, at : at + 8, :]
    if r >= half:
        low = pltpu.roll(low, 64, 1)
    else:
        high = pltpu.roll(high, 64, 1)
    low = jnp.where(jnp.logical_and(lane < 64, mine > 0), low, 0.0)
    high = jnp.where(jnp.logical_and(lane >= 64, mine < count - 1), high, 0.0)
    return low, high


def edge_kernel(field, planes, to_low, to_high, cost):
    lane = lax.broadcasted_iota(jnp.int32, (EZ, 128), 1)
    for ex in range(EX):
        for r, out, shift in ((0, to_low, 0), (EY - 1, to_high, 72)):
            rows = 8 * (ex * EY + r)
            mask = lane % 64 >= 56 if shift else lane % 64 < 8
            total = jnp.zeros((EZ, 128), jnp.float32)
            for j in range(4):
                x = field[rows : rows + 8, 128 * j : 128 * (j + 1)]
                if ex == 0 and j == 0:
                    x = x + neighbours(planes, lane, r)[0]
                if ex == EX - 1 and j == 3:
                    x = x + neighbours(planes, lane, r)[1]
                x = jnp.where(mask, x, 0.0)
                move = (shift + 8 * j) % 128
                total = total + (pltpu.roll(x, move, 1) if move else x)
            out[8 * ex : 8 * (ex + 1), :] = total
    total = planes[0, 4 * EY : 4 * EY + 1, :]
    for other in range(1, planes.shape[0]):
        total = total + planes[other, 4 * EY : 4 * EY + 1, :]
    cost[...] = total


def finish_kernel(field, planes, from_low, from_high, out):
    lane = lax.broadcasted_iota(jnp.int32, (EZ, 128), 1)
    for ex in range(EX):
        for r in range(EY):
            rows = 8 * (ex * EY + r)
            for j in range(4):
                x = field[rows : rows + 8, 128 * j : 128 * (j + 1)]
                if ex == 0 and j == 0:
                    x = x + neighbours(planes, lane, r)[0]
                if ex == EX - 1 and j == 3:
                    x = x + neighbours(planes, lane, r)[1]
                if r == 0:
                    part = from_low[8 * ex : 8 * (ex + 1), :]
                    move = (128 - 8 * j) % 128
                    part = pltpu.roll(part, move, 1) if move else part
                    x = x + jnp.where(lane % 64 < 8, part, 0.0)
                if r == EY - 1:
                    part = from_high[8 * ex : 8 * (ex + 1), :]
                    x = x + jnp.where(lane % 64 >= 56, pltpu.roll(part, 56 - 8 * j, 1), 0.0)
                out[rows : rows + 8, 128 * j : 128 * (j + 1)] = x


def on_device(obs_coord, obs_resid, obs_weight, obs_dest, obs_send_slot, obs_elem, obs_slot):
    peer_count = lax.axis_size("dev")
    group_count = lax.axis_size("grp")
    row_count = obs_resid.shape[0]
    capacity = 2 * row_count // peer_count
    wide = min(256, capacity)
    per_peer = capacity // wide
    message_rows = -(-(FIELDS * per_peer + 1) // 8) * 8
    block = 1024
    f32 = jnp.float32
    flat = [a.reshape(1, row_count) for a in (obs_resid, obs_weight, obs_dest, obs_send_slot, obs_elem)]
    send = pl.pallas_call(
        functools.partial(pack_kernel, capacity=capacity, wide=wide, chunk=512),
        out_shape=jax.ShapeDtypeStruct((peer_count, message_rows, wide), f32),
        scratch_shapes=[pltpu.VMEM((2 * row_count // wide * 8, wide), f32)],
        name="pack",
    )(obs_coord, *flat)
    got = lax.all_to_all(send, "dev", split_axis=0, concat_axis=0, tiled=True)
    field, planes = pl.pallas_call(
        functools.partial(field_kernel, capacity=capacity, wide=wide, block=block),
        out_shape=(
            jax.ShapeDtypeStruct((ELEM_DEV, 512), f32),
            jax.ShapeDtypeStruct((group_count, 4 * EY + 8, 128), f32),
        ),
        scratch_shapes=[
            pltpu.VMEM((ELEM_DEV, 512), f32),
            pltpu.VMEM((ELEM_DEV, block), jnp.bfloat16),
            pltpu.VMEM((512, block), jnp.bfloat16),
            pltpu.VMEM((512, block), jnp.bfloat16),
        ],
        name="field",
    )(got)
    planes = lax.all_to_all(planes, "grp", split_axis=0, concat_axis=0, tiled=True)
    edge = jax.ShapeDtypeStruct((EX * EZ, 128), f32)
    to_low, to_high, cost = pl.pallas_call(
        edge_kernel,
        out_shape=(edge, edge, jax.ShapeDtypeStruct((1, 128), f32)),
        name="edge",
    )(field, planes)
    forward = [(i, i + 1) for i in range(peer_count - 1)]
    backward = [(target, source) for source, target in forward]
    from_low = lax.ppermute(to_high, "dev", forward)
    from_high = lax.ppermute(to_low, "dev", backward)
    nodal = pl.pallas_call(
        finish_kernel,
        out_shape=jax.ShapeDtypeStruct((ELEM_DEV, 512), f32),
        name="finish",
    )(field, planes, from_low, from_high)
    return (nodal.reshape(EX, EY, EZ, 512), cost[0, 0])


def solution(mesh):
    placed = (
        P(None, ("grp", "dev")),
        P(("grp", "dev")),
        P(("grp", "dev")),
        P(("grp", "dev")),
        P(("grp", "dev")),
        P(("grp", "dev")),
        P(("grp", "dev")),
    )
    return jax.shard_map(
        on_device,
        mesh=mesh,
        in_specs=placed,
        out_specs=(P("grp", "dev", None, None), P()),
        check_vma=False,
    )
```

time: 227 us -> 51.7 us (0.23)
  local copies, waits for them, and re-layouts: 111 us -> 0.6 us
  matrix products: 20.7 us -> 0 us
  Pallas kernels: 0 us -> 19.2 us
  blocking collectives: 39.5 us -> 20.7 us
  other arithmetic: 17.6 us -> 0 us
  starting transfers between devices: 22.7 us -> 6.77 us
  waiting for transfers between devices: 13 us -> 3.32 us
    scatter x3 -> x0, local copies, waits for them, and re-layouts: 51.9 us -> none  [the longest x1 23 us: on_device(): packed.at[:, got_cells.reshape(-1)].set(got_values.reshape(channels, -1))]
    psum x1 -> x0, blocking collectives: 39.5 us -> none  [on_device(): total_cost = lax.psum(0.5 * jnp.sum(forcing * obs_resid), ('grp', 'dev'))]
    slice x6 -> x0, local copies, waits for them, and re-layouts: 22.9 us -> none  [the longest x1 14.8 us: on_device(): first_w = basis_values(packed[0]) * packed[3]]
    all_to_all x0 -> x2, blocking collectives: none -> 20.7 us  [the longest x1 13 us: on_device(): got = lax.all_to_all(send, 'dev', split_axis=0, concat_axis=0, tiled=True)]
    dot_general x1 -> x0, matrix products: 20.7 us -> none  [contract(): jnp.einsum('aes,kes->eak', outer, third, precision=lax.Precision.HIGHEST)]
    pallas_call x0 -> x4, Pallas kernels: none -> 19.2 us  [the longest x1 10.3 us: on_device(): pl.pallas_call(functools.partial(field_kernel, capacity=capacity, wide=wi...]
    unnamed x6 -> x4, local copies, waits for them, and re-layouts: 14.4 us -> 0.6 us
    all_to_all x2 -> x0, starting transfers between devices: 11.2 us -> none  [the longest x1 6.37 us: on_device(): lax.all_to_all(send_cells, 'dev', split_axis=1, concat_axis=1, tiled=True)]
  transfers between devices with their start and end apart: 6 -> 2, of which waited for: 3 -> 1; matrix products, arithmetic and copies ran while one was open for 12% -> 0% of each run, Pallas kernels for 0% -> 0%
where the time goes in v1:
time: 51.7 us; the launch traced here: 51.2 us
  blocking collectives  20.7 us (40%)
  Pallas kernels  19.2 us (37%)
  starting transfers between devices  6.77 us (13%)
  waiting for transfers between devices  3.32 us (6%)
  between operations  0.67 us (1%)
  local copies, waits for them, and re-layouts  0.6 us (1%)
    all_to_all x1, blocking collectives, on_device(): got = lax.all_to_all(send, 'dev', split_axis=0, concat_axis=0, tiled=True)  13 us
    pallas_call x1, Pallas kernels, on_device(): pl.pallas_call(functools.partial(field_kernel, capacity=capacity, wide=wi...  10.3 us
    all_to_all x1, blocking collectives, on_device(): lax.all_to_all(planes, 'grp', split_axis=0, concat_axis=0, tiled=True)  7.71 us
    pallas_call x1, Pallas kernels, on_device(): pl.pallas_call(functools.partial(pack_kernel, capacity=capacity, wide=wid...  5.04 us
    ppermute x1, starting transfers between devices, on_device(): from_low = lax.ppermute(to_high, 'dev', forward)  4.85 us
    ppermute x1, waiting for transfers between devices, on_device(): from_high = lax.ppermute(to_low, 'dev', backward)  3.32 us
    pallas_call x1, Pallas kernels, on_device(): pl.pallas_call(finish_kernel, out_shape=jax.ShapeDtypeStruct((ELEM_DEV, 5...  1.99 us
    ppermute x1, starting transfers between devices, on_device(): from_high = lax.ppermute(to_low, 'dev', backward)  1.92 us
  transfers between devices with their start and end apart: 2, of which 1 were waited for; matrix products, arithmetic and copies ran while one was open for 0% of the time, Pallas kernels for 0%

profile of v1, /device:TPU:1, one launch (start us, length us, event | category | flops | bytes accessed | tf_op | source)
XLA Modules:
  0.0 51.2 jit_solution(3069683517438458256)
XLA Ops:
  0.6 5.0 %pack.1 = f32[8,24,256]{2,1,0:T(8,128)} custom-call(f32[3,4096]{1,0:T(4,128)} %coord.1, f32[1,4096]{1,0:T(1,128)} %bitcast.9, f32[1,4096]{1,0:T(1,128)} %bitcast.10, s32[1,4096]{1,0:T(1,128)} %bitcast.11, s32[1,4096]{1,0:T(1,128)} %bitcast.12, s32[1,4096]{1,0:T(1,128)} %bitcast.13), custom_call_target="tpu_custom_call" | custom-call | tf_op jit(solution)/shard_map/pack/pallas_call | solution.py:248
  5.7 13.0 %all_to_all.10.got = f32[8,24,256]{2,1,0:T(8,128)} all-to-all(f32[8,24,256]{2,1,0:T(8,128)} %pack.1), channel_id=1, replica_groups=mesh['grp'=4,'dev'=8] {'dev'}, dimensions={0} | all-to-all | bytes 393216 | tf_op jit(solution)/shard_map/all_to_all | solution.py:254
  18.7 10.3 %field.1 = (f32[256,512]{1,0:T(8,128)}, f32[4,40,128]{2,1,0:T(8,128)}) custom-call(f32[8,24,256]{2,1,0:T(8,128)} %all_to_all.10.got), custom_call_target="tpu_custom_call" | custom-call | tf_op jit(solution)/shard_map/field/pallas_call | solution.py:255
  29.0 7.7 %all_to_all.11.planes = f32[4,40,128]{2,1,0:T(8,128)} all-to-all(f32[4,40,128]{2,1,0:T(8,128)} %get-tuple-element.8), channel_id=1, replica_groups=mesh['grp'=4,'dev'=8] {'grp'}, dimensions={0} | all-to-all | bytes 163840 | tf_op jit(solution)/shard_map/all_to_all | solution.py:269
  36.7 1.8 %edge.1 = (f32[32,128]{1,0:T(8,128)}, f32[32,128]{1,0:T(8,128)}, f32[1,128]{1,0:T(1,128)}) custom-call(f32[256,512]{1,0:T(8,128)} %get-tuple-element.7.field, f32[4,40,128]{2,1,0:T(8,128)} %all_to_all.11.planes), custom_call_target="tpu_custom_call" | custom-call | tf_op jit(solution)/shard_map/edge/pallas_call | solution.py:271
  38.5 4.8 %collective-permute-start = (f32[32,128]{1,0:T(8,128)}, f32[32,128]{1,0:T(8,128)S(1)}, u32[]{:S(2)}, u32[]{:S(2)}) collective-permute-start(f32[32,128]{1,0:T(8,128)} %get-tuple-element.9), channel_id=1, source_target_pairs={{0,1},{1,2},{2,3},{3,4},{4,5},{5,6},{6,7},{8,9},{9,10},{10,11},{11... | collective-permute-start | bytes 49160 | tf_op jit(solution)/shard_map/ppermute | solution.py:278
  43.4 1.9 %collective-permute-start.1 = (f32[32,128]{1,0:T(8,128)}, f32[32,128]{1,0:T(8,128)S(1)}, u32[]{:S(2)}, u32[]{:S(2)}) collective-permute-start(f32[32,128]{1,0:T(8,128)} %get-tuple-element.10), channel_id=1, source_target_pairs={{1,0},{2,1},{3,2},{4,3},{5,4},{6,5},{7,6},{9,8},{10,9},{11,10},{12... | collective-permute-start | bytes 49160 | tf_op jit(solution)/shard_map/ppermute | solution.py:279
  45.3 0.0 collective-permute-done.from_low
  45.3 0.0 copy-start
  45.3 3.3 %collective-permute-done.1.from_high = f32[32,128]{1,0:T(8,128)S(1)} collective-permute-done((f32[32,128]{1,0:T(8,128)}, f32[32,128]{1,0:T(8,128)S(1)}, u32[]{:S(2)}, u32[]{:S(2)}) %collective-permute-start.1) | collective-permute-done | bytes 16416 | tf_op jit(solution)/shard_map/ppermute | solution.py:279
  48.6 0.0 copy-done
  48.6 0.0 copy-start.1
  48.6 0.6 %copy-done.1 = f32[32,128]{1,0:T(8,128)} copy-done((f32[32,128]{1,0:T(8,128)}, f32[32,128]{1,0:T(8,128)S(1)}, u32[]{:S(2)}) %copy-start.1) | copy-done | bytes 16408
  49.2 2.0 %finish.1 = f32[256,512]{1,0:T(8,128)} custom-call(f32[256,512]{1,0:T(8,128)} %get-tuple-element.7.field, f32[4,40,128]{2,1,0:T(8,128)} %all_to_all.11.planes, f32[32,128]{1,0:T(8,128)} %copy-done, f32[32,128]{1,0:T(8,128)} %copy-done.1), custom_call_target="tpu_custom_call" | custom-call | tf_op jit(solution)/shard_map/finish/pallas_call | solution.py:280
Async XLA Ops:
  38.5 6.8 %collective-permute-start = (f32[32,128]{1,0:T(8,128)}, f32[32,128]{1,0:T(8,128)S(1)}, u32[]{:S(2)}, u32[]{:S(2)}) collective-permute-start(f32[32,128]{1,0:T(8,128)} %get-tuple-element.9), channel_id=1, source_target_pairs={{0,1},{1,2},{2,3},{3,4},{4,5},{5,6},{6,7},{8,9},{9,10},{10,11},{11... | collective-permute-start | bytes 49160 | tf_op jit(solution)/shard_map/ppermute | solution.py:278
  43.4 5.3 %collective-permute-start.1 = (f32[32,128]{1,0:T(8,128)}, f32[32,128]{1,0:T(8,128)S(1)}, u32[]{:S(2)}, u32[]{:S(2)}) collective-permute-start(f32[32,128]{1,0:T(8,128)} %get-tuple-element.10), channel_id=1, source_target_pairs={{1,0},{2,1},{3,2},{4,3},{5,4},{6,5},{7,6},{9,8},{10,9},{11,10},{12... | collective-permute-start | bytes 49160 | tf_op jit(solution)/shard_map/ppermute | solution.py:279
  45.3 3.3 %copy-start = (f32[32,128]{1,0:T(8,128)}, f32[32,128]{1,0:T(8,128)S(1)}, u32[]{:S(2)}) copy-start(f32[32,128]{1,0:T(8,128)S(1)} %collective-permute-done.from_low) | copy-start | bytes 49156
  48.6 0.6 %copy-start.1 = (f32[32,128]{1,0:T(8,128)}, f32[32,128]{1,0:T(8,128)S(1)}, u32[]{:S(2)}) copy-start(f32[32,128]{1,0:T(8,128)S(1)} %collective-permute-done.1.from_high) | copy-start | bytes 49156

commit v2 on v1

--- a/solution.py
+++ b/solution.py
@@ -14,6 +14,7 @@
 ELEM_DEV = 256
 NODES = 8
 FIELDS = 5
+PIECES = 3
 ANCHORS = [-math.cos(math.pi * k / 7) for k in range(NODES)]
 SCALES = [
     1.0 / math.prod(ANCHORS[i] - ANCHORS[m] for m in range(NODES) if m != i) for i in range(NODES)
@@ -35,6 +36,7 @@
     high_count = 2 * rows // wide
     acc[...] = jnp.zeros_like(acc)
     lane_ids = lax.broadcasted_iota(jnp.int32, (wide, chunk), 0)
+    high_ids = lax.broadcasted_iota(jnp.int32, (high_count, chunk), 0)
 
     def step(i, cost):
         at = pl.ds(pl.multiple_of(i * chunk, chunk), chunk)
@@ -44,34 +46,33 @@
         high = target // wide
         low = target - high * wide
         right = jnp.where(lane_ids == low, 1.0, 0.0).astype(jnp.bfloat16)
-        values = jnp.concatenate(
+        chosen = high_ids == high
+        pieces = pieces_of(jnp.concatenate([coord[:, at], forcing], axis=0))
+        lines = [piece[k : k + 1, :] for k in range(FIELDS - 1) for piece in pieces]
+        lines.append(elem[:, at].astype(jnp.float32))
+        left = jnp.concatenate(
             [
-                coord[:, at],
-                forcing,
-                elem[:, at].astype(jnp.float32),
-                jnp.zeros((8 - FIELDS, chunk), jnp.float32),
+                jnp.where(chosen, jnp.broadcast_to(line, chosen.shape), 0.0).astype(jnp.bfloat16)
+                for line in lines
             ],
             axis=0,
         )
-        high_rep = jnp.broadcast_to(high, (8, chunk))
-        pieces = pieces_of(values)
-        total = None
-        for piece in pieces:
-            left = jnp.concatenate(
-                [jnp.where(high_rep == h, piece, 0.0) for h in range(high_count)], axis=0
-            ).astype(jnp.bfloat16)
-            part = lax.dot_general(left, right, NT, preferred_element_type=jnp.float32)
-            total = part if total is None else total + part
-        acc[...] += total
+        acc[...] += lax.dot_general(left, right, NT, preferred_element_type=jnp.float32)
         return cost + forcing * residual
 
     cost = lax.fori_loop(0, rows // chunk, step, jnp.zeros((1, chunk), jnp.float32))
     cost = 0.5 * jnp.sum(cost, axis=1, keepdims=True)
     used = FIELDS * per_peer
+    for k in range(FIELDS):
+        base = k * PIECES * high_count
+        total = acc[base : base + high_count, :]
+        for p in range(1, PIECES if k < FIELDS - 1 else 1):
+            total = total + acc[base + p * high_count : base + (p + 1) * high_count, :]
+        for peer in range(out.shape[0]):
+            out[peer, k * per_peer : (k + 1) * per_peer, :] = total[
+                peer * per_peer : (peer + 1) * per_peer, :
+            ]
     for peer in range(out.shape[0]):
-        for j in range(per_peer):
-            source = (peer * per_peer + j) * 8
-            out[peer, FIELDS * j : FIELDS * (j + 1), :] = acc[source : source + FIELDS, :]
         out[peer, used:, :] = jnp.broadcast_to(cost, (out.shape[1] - used, wide))
 
 
@@ -82,7 +83,7 @@
     return factor
 
 
-def field_kernel(got, field, planes, acc, elems, first, second, *, capacity, wide, block):
+def field_kernel(got, field, planes, acc, raw, elems, outer, *, capacity, wide, block):
     peer_count = got.shape[0]
     per_peer = capacity // wide
     parts = block // wide
@@ -96,8 +97,10 @@
     def step(i, carry):
         for q in range(parts):
             peer = i * (parts // per_peer) + q // per_peer
-            row = FIELDS * (q % per_peer)
-            u, v, w, f, e = (got[peer, row + k : row + k + 1, :] for k in range(FIELDS))
+            row = q % per_peer
+            u, v, w, f, e = (
+                got[peer, row + k * per_peer : row + k * per_peer + 1, :] for k in range(FIELDS)
+            )
             lanes = slice(q * wide, (q + 1) * wide)
             elems[:, lanes] = jnp.where(elem_ids == e, 1.0, 0.0).astype(jnp.bfloat16)
             first_w = basis_of(u, node, scale) * f
@@ -108,16 +111,16 @@
                 mine = jnp.broadcast_to(first_w[a : a + 1, :], (NODES, wide))
                 whole = jnp.concatenate([mine * inner[b] for b in range(NODES)], axis=0)
                 head = whole.astype(jnp.bfloat16)
-                at = slice(64 * a, 64 * (a + 1))
-                first[at, lanes] = head
-                second[at, lanes] = (whole - head.astype(jnp.float32)).astype(jnp.bfloat16)
-        chosen = elems[...]
+                rest = (whole - head.astype(jnp.float32)).astype(jnp.bfloat16)
+                outer[64 * a : 64 * (a + 1), lanes] = head
+                outer[512 + 64 * a : 512 + 64 * (a + 1), lanes] = rest
         acc[...] += lax.dot_general(
-            chosen, first[...], NT, preferred_element_type=jnp.float32
-        ) + lax.dot_general(chosen, second[...], NT, preferred_element_type=jnp.float32)
+            outer[...], elems[...], NT, preferred_element_type=jnp.float32
+        )
         return carry
 
     lax.fori_loop(0, peer_count * capacity // block, step, 0)
+    raw[...] = (acc[:512] + acc[512:]).T
 
     lane = lax.broadcasted_iota(jnp.int32, (EZ, 128), 1)
     level = lax.broadcasted_iota(jnp.int32, (EZ, 128), 0)
@@ -127,7 +130,7 @@
     for j in range(4):
         blocks = []
         for r in range(EX * EY):
-            x = acc[8 * r : 8 * (r + 1), 128 * j : 128 * (j + 1)]
+            x = raw[8 * r : 8 * (r + 1), 128 * j : 128 * (j + 1)]
             up = pltpu.roll(pltpu.roll(x, EZ - 1, 0), 7, 1)
             down = pltpu.roll(pltpu.roll(x, 1, 0), 121, 1)
             blocks.append(x + jnp.where(take_up, up, 0.0) + jnp.where(take_down, down, 0.0))
@@ -234,6 +237,10 @@
                 out[rows : rows + 8, 128 * j : 128 * (j + 1)] = x
 
 
+def in_vmem(array):
+    return pltpu.with_memory_space_constraint(array, pltpu.VMEM)
+
+
 def on_device(obs_coord, obs_resid, obs_weight, obs_dest, obs_send_slot, obs_elem, obs_slot):
     peer_count = lax.axis_size("dev")
     group_count = lax.axis_size("grp")
@@ -242,32 +249,34 @@
     wide = min(256, capacity)
     per_peer = capacity // wide
     message_rows = -(-(FIELDS * per_peer + 1) // 8) * 8
-    block = 1024
+    block = 2 * row_count
+    lines = (FIELDS - 1) * PIECES + 1
     f32 = jnp.float32
     flat = [a.reshape(1, row_count) for a in (obs_resid, obs_weight, obs_dest, obs_send_slot, obs_elem)]
     send = pl.pallas_call(
-        functools.partial(pack_kernel, capacity=capacity, wide=wide, chunk=512),
-        out_shape=jax.ShapeDtypeStruct((peer_count, message_rows, wide), f32),
-        scratch_shapes=[pltpu.VMEM((2 * row_count // wide * 8, wide), f32)],
+        functools.partial(pack_kernel, capacity=capacity, wide=wide, chunk=row_count),
+        out_shape=pltpu.VMEM((peer_count, message_rows, wide), f32),
+        scratch_shapes=[pltpu.VMEM((lines * 2 * row_count // wide, wide), f32)],
         name="pack",
     )(obs_coord, *flat)
     got = lax.all_to_all(send, "dev", split_axis=0, concat_axis=0, tiled=True)
     field, planes = pl.pallas_call(
         functools.partial(field_kernel, capacity=capacity, wide=wide, block=block),
         out_shape=(
-            jax.ShapeDtypeStruct((ELEM_DEV, 512), f32),
-            jax.ShapeDtypeStruct((group_count, 4 * EY + 8, 128), f32),
+            pltpu.VMEM((ELEM_DEV, 512), f32),
+            pltpu.VMEM((group_count, 4 * EY + 8, 128), f32),
         ),
         scratch_shapes=[
+            pltpu.VMEM((2 * 512, ELEM_DEV), f32),
             pltpu.VMEM((ELEM_DEV, 512), f32),
             pltpu.VMEM((ELEM_DEV, block), jnp.bfloat16),
-            pltpu.VMEM((512, block), jnp.bfloat16),
-            pltpu.VMEM((512, block), jnp.bfloat16),
+            pltpu.VMEM((2 * 512, block), jnp.bfloat16),
         ],
         name="field",
-    )(got)
+    )(in_vmem(got))
     planes = lax.all_to_all(planes, "grp", split_axis=0, concat_axis=0, tiled=True)
-    edge = jax.ShapeDtypeStruct((EX * EZ, 128), f32)
+    edge = pltpu.VMEM((EX * EZ, 128), f32)
+    field, planes = in_vmem(field), in_vmem(planes)
     to_low, to_high, cost = pl.pallas_call(
         edge_kernel,
         out_shape=(edge, edge, jax.ShapeDtypeStruct((1, 128), f32)),
@@ -281,7 +290,7 @@
         finish_kernel,
         out_shape=jax.ShapeDtypeStruct((ELEM_DEV, 512), f32),
         name="finish",
-    )(field, planes, from_low, from_high)
+    )(field, planes, in_vmem(from_low), in_vmem(from_high))
     return (nodal.reshape(EX, EY, EZ, 512), cost[0, 0])
 
 

time: 51.7 us -> 39.7 us (0.77)
  Pallas kernels: 19.2 us -> 8.96 us
  blocking collectives: 20.7 us -> 19.7 us
  local copies, waits for them, and re-layouts: 0.6 us -> 0 us
    pallas_call x1, Pallas kernels: 10.3 us -> 5.46 us  [on_device(): pl.pallas_call(functools.partial(field_kernel, capacity=capacity, wide=wi...]
    pallas_call x1, Pallas kernels: 5.04 us -> 2.01 us  [on_device(): pl.pallas_call(functools.partial(pack_kernel, capacity=capacity, wide=wid...]
    pallas_call x1, Pallas kernels: 1.81 us -> 0.59 us  [on_device(): pl.pallas_call(edge_kernel, out_shape=(edge, edge, jax.ShapeDtypeStruct((...]
    pallas_call x1, Pallas kernels: 1.99 us -> 0.9 us  [on_device(): pl.pallas_call(finish_kernel, out_shape=jax.ShapeDtypeStruct((ELEM_DEV, 5...]
    all_to_all x1, blocking collectives: 7.71 us -> 6.98 us  [on_device(): lax.all_to_all(planes, 'grp', split_axis=0, concat_axis=0, tiled=True)]
    unnamed x4 -> x0, local copies, waits for them, and re-layouts: 0.6 us -> none
where the time goes in v2:
time: 39.7 us; the launch traced here: 39.5 us
  blocking collectives  19.7 us (50%)
  Pallas kernels  8.96 us (23%)
  starting transfers between devices  7.04 us (18%)
  waiting for transfers between devices  3.12 us (8%)
  between operations  0.67 us (2%)
    all_to_all x1, blocking collectives, on_device(): got = lax.all_to_all(send, 'dev', split_axis=0, concat_axis=0, tiled=True)  12.7 us
    all_to_all x1, blocking collectives, on_device(): lax.all_to_all(planes, 'grp', split_axis=0, concat_axis=0, tiled=True)  6.98 us
    pallas_call x1, Pallas kernels, on_device(): pl.pallas_call(functools.partial(field_kernel, capacity=capacity, wide=wi...  5.46 us
    ppermute x1, starting transfers between devices, on_device(): from_low = lax.ppermute(to_high, 'dev', forward)  5.12 us
    ppermute x1, waiting for transfers between devices, on_device(): from_high = lax.ppermute(to_low, 'dev', backward)  3.12 us
    pallas_call x1, Pallas kernels, on_device(): pl.pallas_call(functools.partial(pack_kernel, capacity=capacity, wide=wid...  2.01 us
    ppermute x1, starting transfers between devices, on_device(): from_high = lax.ppermute(to_low, 'dev', backward)  1.92 us
    pallas_call x1, Pallas kernels, on_device(): pl.pallas_call(finish_kernel, out_shape=jax.ShapeDtypeStruct((ELEM_DEV, 5...  0.9 us
  transfers between devices with their start and end apart: 2, of which 1 were waited for; matrix products, arithmetic and copies ran while one was open for 0% of the time, Pallas kernels for 0%

profile of v2, /device:TPU:1, one launch (start us, length us, event | category | flops | bytes accessed | tf_op | source)
XLA Modules:
  0.0 39.5 jit_solution(17074716299450565302)
XLA Ops:
  0.6 2.0 %pack.1 = f32[8,24,256]{2,1,0:T(8,128)S(1)} custom-call(f32[3,4096]{1,0:T(4,128)} %coord.1, f32[1,4096]{1,0:T(1,128)} %bitcast.9, f32[1,4096]{1,0:T(1,128)} %bitcast.10, s32[1,4096]{1,0:T(1,128)} %bitcast.11, s32[1,4096]{1,0:T(1,128)} %bitcast.12, s32[1,4096]{1,0:T(1,128)} %bitcast.13), custom_call_target="tpu_custom_call" | custom-call | tf_op jit(solution)/shard_map/pack/pallas_call | solution.py:256
  2.6 12.7 %all_to_all.10.got = f32[8,24,256]{2,1,0:T(8,128)S(1)} all-to-all(f32[8,24,256]{2,1,0:T(8,128)S(1)} %pack.1), channel_id=1, replica_groups=mesh['grp'=4,'dev'=8] {'dev'}, dimensions={0} | all-to-all | bytes 393216 | tf_op jit(solution)/shard_map/all_to_all | solution.py:262
  15.3 5.5 %field.1 = (f32[256,512]{1,0:T(8,128)S(1)}, f32[4,40,128]{2,1,0:T(8,128)S(1)}) custom-call(f32[8,24,256]{2,1,0:T(8,128)S(1)} %all_to_all.10.got), custom_call_target="tpu_custom_call" | custom-call | tf_op jit(solution)/shard_map/field/pallas_call | solution.py:263
  20.8 7.0 %all_to_all.11.planes = f32[4,40,128]{2,1,0:T(8,128)S(1)} all-to-all(f32[4,40,128]{2,1,0:T(8,128)S(1)} %get-tuple-element.8), channel_id=1, replica_groups=mesh['grp'=4,'dev'=8] {'grp'}, dimensions={0} | all-to-all | bytes 163840 | tf_op jit(solution)/shard_map/all_to_all | solution.py:277
  27.8 0.6 %edge.1 = (f32[32,128]{1,0:T(8,128)S(1)}, f32[32,128]{1,0:T(8,128)S(1)}, f32[1,128]{1,0:T(1,128)}) custom-call(f32[256,512]{1,0:T(8,128)S(1)} %get-tuple-element.7.field, f32[4,40,128]{2,1,0:T(8,128)S(1)} %all_to_all.11.planes), custom_call_target="tpu_custom_call" | custom-call | tf_op jit(solution)/shard_map/edge/pallas_call | solution.py:280
  28.4 5.1 %collective-permute-start = (f32[32,128]{1,0:T(8,128)S(1)}, f32[32,128]{1,0:T(8,128)S(1)}, u32[]{:S(2)}, u32[]{:S(2)}) collective-permute-start(f32[32,128]{1,0:T(8,128)S(1)} %get-tuple-element.9), channel_id=1, source_target_pairs={{0,1},{1,2},{2,3},{3,4},{4,5},{5,6},{6,7},{8,9},{9,10},{10,11},{11... | collective-permute-start | bytes 49160 | tf_op jit(solution)/shard_map/ppermute | solution.py:287
  33.5 1.9 %collective-permute-start.1 = (f32[32,128]{1,0:T(8,128)S(1)}, f32[32,128]{1,0:T(8,128)S(1)}, u32[]{:S(2)}, u32[]{:S(2)}) collective-permute-start(f32[32,128]{1,0:T(8,128)S(1)} %get-tuple-element.10), channel_id=1, source_target_pairs={{1,0},{2,1},{3,2},{4,3},{5,4},{6,5},{7,6},{9,8},{10,9},{11,10},{12... | collective-permute-start | bytes 49160 | tf_op jit(solution)/shard_map/ppermute | solution.py:288
  35.4 0.0 collective-permute-done.from_low
  35.4 3.1 %collective-permute-done.1.from_high = f32[32,128]{1,0:T(8,128)S(1)} collective-permute-done((f32[32,128]{1,0:T(8,128)S(1)}, f32[32,128]{1,0:T(8,128)S(1)}, u32[]{:S(2)}, u32[]{:S(2)}) %collective-permute-start.1) | collective-permute-done | bytes 16416 | tf_op jit(solution)/shard_map/ppermute | solution.py:288
  38.6 0.9 %finish.1 = f32[256,512]{1,0:T(8,128)} custom-call(f32[256,512]{1,0:T(8,128)S(1)} %get-tuple-element.7.field, f32[4,40,128]{2,1,0:T(8,128)S(1)} %all_to_all.11.planes, f32[32,128]{1,0:T(8,128)S(1)} %collective-permute-done.from_low, f32[32,128]{1,0:T(8,128)S(1)} %collective-permute-done.1.from_high), custom_call_target="tpu_custom_call" | custom-call | tf_op jit(solution)/shard_map/finish/pallas_call | solution.py:289
Async XLA Ops:
  28.4 7.1 %collective-permute-start = (f32[32,128]{1,0:T(8,128)S(1)}, f32[32,128]{1,0:T(8,128)S(1)}, u32[]{:S(2)}, u32[]{:S(2)}) collective-permute-start(f32[32,128]{1,0:T(8,128)S(1)} %get-tuple-element.9), channel_id=1, source_target_pairs={{0,1},{1,2},{2,3},{3,4},{4,5},{5,6},{6,7},{8,9},{9,10},{10,11},{11... | collective-permute-start | bytes 49160 | tf_op jit(solution)/shard_map/ppermute | solution.py:287
  33.5 5.1 %collective-permute-start.1 = (f32[32,128]{1,0:T(8,128)S(1)}, f32[32,128]{1,0:T(8,128)S(1)}, u32[]{:S(2)}, u32[]{:S(2)}) collective-permute-start(f32[32,128]{1,0:T(8,128)S(1)} %get-tuple-element.10), channel_id=1, source_target_pairs={{1,0},{2,1},{3,2},{4,3},{5,4},{6,5},{7,6},{9,8},{10,9},{11,10},{12... | collective-permute-start | bytes 49160 | tf_op jit(solution)/shard_map/ppermute | solution.py:288

commit v3 on v2

--- a/solution.py
+++ b/solution.py
@@ -83,7 +83,7 @@
     return factor
 
 
-def field_kernel(got, field, planes, acc, raw, elems, outer, *, capacity, wide, block):
+def field_kernel(got, field, to_below, to_above, cost, acc, raw, elems, outer, *, capacity, wide, block):
     peer_count = got.shape[0]
     per_peer = capacity // wide
     parts = block // wide
@@ -156,33 +156,31 @@
         field[8 * r : 8 * (r + 1), 0:128] = x
         field[8 * r : 8 * (r + 1), 384:512] = y
     half = EY // 2
-    mine = lax.axis_index("grp")
     used = FIELDS * per_peer
-    cost = got[0, used : used + 1, 0:128]
+    total = got[0, used : used + 1, 0:128]
     for peer in range(1, peer_count):
-        cost = cost + got[peer, used : used + 1, 0:128]
+        total = total + got[peer, used : used + 1, 0:128]
+    total = jnp.broadcast_to(total, (8, 128))
     last = (EX - 1) * EY
     for r in range(half):
-        low_pack = jnp.where(lane < 64, lower[r], pltpu.roll(lower[r + half], 64, 1))
-        high_pack = jnp.where(
+        to_below[8 * r : 8 * (r + 1), :] = jnp.where(
+            lane < 64, lower[r], pltpu.roll(lower[r + half], 64, 1)
+        )
+        to_above[8 * r : 8 * (r + 1), :] = jnp.where(
             lane < 64, pltpu.roll(upper[last + r], 64, 1), upper[last + r + half]
         )
-        for other in range(planes.shape[0]):
-            message = jnp.where(other == mine - 1, low_pack, 0.0)
-            planes[other, 8 * r : 8 * (r + 1), :] = jnp.where(other == mine + 1, high_pack, message)
-    for other in range(planes.shape[0]):
-        planes[other, 8 * half :, :] = jnp.broadcast_to(cost, (8, 128))
-
-
-def neighbours(planes, lane, r):
-    count = planes.shape[0]
+    to_below[8 * half :, :] = total
+    to_above[8 * half :, :] = total
+    cost[...] = total
+
+
+def neighbours(from_below, from_above, lane, r):
+    count = lax.axis_size("grp")
     half = EY // 2
     mine = lax.axis_index("grp")
-    below = jnp.maximum(mine - 1, 0)
-    above = jnp.minimum(mine + 1, count - 1)
     at = 8 * (r % half)
-    low = planes[below, at : at + 8, :]
-    high = planes[above, at : at + 8, :]
+    low = from_below[at : at + 8, :]
+    high = from_above[at : at + 8, :]
     if r >= half:
         low = pltpu.roll(low, 64, 1)
     else:
@@ -192,7 +190,8 @@
     return low, high
 
 
-def edge_kernel(field, planes, to_low, to_high, cost):
+def edge_kernel(field, from_below, from_above, *rest):
+    *costs, to_low, to_high, cost = rest
     lane = lax.broadcasted_iota(jnp.int32, (EZ, 128), 1)
     for ex in range(EX):
         for r, out, shift in ((0, to_low, 0), (EY - 1, to_high, 72)):
@@ -202,20 +201,27 @@
             for j in range(4):
                 x = field[rows : rows + 8, 128 * j : 128 * (j + 1)]
                 if ex == 0 and j == 0:
-                    x = x + neighbours(planes, lane, r)[0]
+                    x = x + neighbours(from_below, from_above, lane, r)[0]
                 if ex == EX - 1 and j == 3:
-                    x = x + neighbours(planes, lane, r)[1]
+                    x = x + neighbours(from_below, from_above, lane, r)[1]
                 x = jnp.where(mask, x, 0.0)
                 move = (shift + 8 * j) % 128
                 total = total + (pltpu.roll(x, move, 1) if move else x)
             out[8 * ex : 8 * (ex + 1), :] = total
-    total = planes[0, 4 * EY : 4 * EY + 1, :]
-    for other in range(1, planes.shape[0]):
-        total = total + planes[other, 4 * EY : 4 * EY + 1, :]
+    count = lax.axis_size("grp")
+    mine = lax.axis_index("grp")
+    row = slice(4 * EY, 4 * EY + 1)
+    known = [costs[0][0:1, :], from_below[row, :], from_above[row, :]]
+    known += [other[0:1, :] for other in costs[1:]]
+    shifts = [0, count - 1, 1] + list(range(2, count - 1))
+    total = jnp.zeros((1, 128), jnp.float32)
+    for group in range(count):
+        for shift, value in zip(shifts, known):
+            total = total + jnp.where((mine + shift) % count == group, value, 0.0)
     cost[...] = total
 
 
-def finish_kernel(field, planes, from_low, from_high, out):
+def finish_kernel(field, from_below, from_above, from_low, from_high, out):
     lane = lax.broadcasted_iota(jnp.int32, (EZ, 128), 1)
     for ex in range(EX):
         for r in range(EY):
@@ -223,9 +229,9 @@
             for j in range(4):
                 x = field[rows : rows + 8, 128 * j : 128 * (j + 1)]
                 if ex == 0 and j == 0:
-                    x = x + neighbours(planes, lane, r)[0]
+                    x = x + neighbours(from_below, from_above, lane, r)[0]
                 if ex == EX - 1 and j == 3:
-                    x = x + neighbours(planes, lane, r)[1]
+                    x = x + neighbours(from_below, from_above, lane, r)[1]
                 if r == 0:
                     part = from_low[8 * ex : 8 * (ex + 1), :]
                     move = (128 - 8 * j) % 128
@@ -239,6 +245,10 @@
 
 def in_vmem(array):
     return pltpu.with_memory_space_constraint(array, pltpu.VMEM)
+
+
+def ring(array, count, shift):
+    return lax.ppermute(array, "grp", [(i, (i + shift) % count) for i in range(count)])
 
 
 def on_device(obs_coord, obs_resid, obs_weight, obs_dest, obs_send_slot, obs_elem, obs_slot):
@@ -260,11 +270,14 @@
         name="pack",
     )(obs_coord, *flat)
     got = lax.all_to_all(send, "dev", split_axis=0, concat_axis=0, tiled=True)
-    field, planes = pl.pallas_call(
+    plane = pltpu.VMEM((4 * EY + 8, 128), f32)
+    field, to_below, to_above, part = pl.pallas_call(
         functools.partial(field_kernel, capacity=capacity, wide=wide, block=block),
         out_shape=(
             pltpu.VMEM((ELEM_DEV, 512), f32),
-            pltpu.VMEM((group_count, 4 * EY + 8, 128), f32),
+            plane,
+            plane,
+            pltpu.VMEM((8, 128), f32),
         ),
         scratch_shapes=[
             pltpu.VMEM((2 * 512, ELEM_DEV), f32),
@@ -274,14 +287,18 @@
         ],
         name="field",
     )(in_vmem(got))
-    planes = lax.all_to_all(planes, "grp", split_axis=0, concat_axis=0, tiled=True)
+    from_below, from_above = (
+        in_vmem(ring(to_below_or_above, group_count, shift))
+        for to_below_or_above, shift in ((to_above, 1), (to_below, group_count - 1))
+    )
+    others = [in_vmem(ring(part, group_count, group_count - k)) for k in range(2, group_count - 1)]
+    field, part = in_vmem(field), in_vmem(part)
     edge = pltpu.VMEM((EX * EZ, 128), f32)
-    field, planes = in_vmem(field), in_vmem(planes)
     to_low, to_high, cost = pl.pallas_call(
         edge_kernel,
         out_shape=(edge, edge, jax.ShapeDtypeStruct((1, 128), f32)),
         name="edge",
-    )(field, planes)
+    )(field, from_below, from_above, part, *others)
     forward = [(i, i + 1) for i in range(peer_count - 1)]
     backward = [(target, source) for source, target in forward]
     from_low = lax.ppermute(to_high, "dev", forward)
@@ -290,7 +307,7 @@
         finish_kernel,
         out_shape=jax.ShapeDtypeStruct((ELEM_DEV, 512), f32),
         name="finish",
-    )(field, planes, in_vmem(from_low), in_vmem(from_high))
+    )(field, from_below, from_above, in_vmem(from_low), in_vmem(from_high))
     return (nodal.reshape(EX, EY, EZ, 512), cost[0, 0])
 
 

time: 39.7 us -> 37.9 us (0.955)
  blocking collectives: 19.7 us -> 12.7 us
  starting transfers between devices: 7.04 us -> 11 us
  waiting for transfers between devices: 3.12 us -> 4.34 us
    all_to_all x1 -> x0, blocking collectives: 6.98 us -> none  [on_device(): lax.all_to_all(planes, 'grp', split_axis=0, concat_axis=0, tiled=True)]
    ppermute x0 -> x3, starting transfers between devices: none -> 3.66 us  [ring(): lax.ppermute(array, 'grp', [(i, (i + shift) % count) for i in range(count)])]
    ppermute x0 -> x3, waiting for transfers between devices: none -> 1.22 us  [ring(): lax.ppermute(array, 'grp', [(i, (i + shift) % count) for i in range(count)])]
  transfers between devices with their start and end apart: 2 -> 5, of which waited for: 1 -> 2; matrix products, arithmetic and copies ran while one was open for 0% -> 0% of each run, Pallas kernels for 0% -> 0%
where the time goes in v3:
time: 37.9 us; the launch traced here: 37.7 us
  blocking collectives  12.7 us (34%)
  starting transfers between devices  11 us (29%)
  Pallas kernels  8.96 us (24%)
  waiting for transfers between devices  4.34 us (11%)
  between operations  0.67 us (2%)
    all_to_all x1, blocking collectives, on_device(): got = lax.all_to_all(send, 'dev', split_axis=0, concat_axis=0, tiled=True)  12.7 us
    pallas_call x1, Pallas kernels, on_device(): pl.pallas_call(functools.partial(field_kernel, capacity=capacity, wide=wi...  5.46 us
    ppermute x1, starting transfers between devices, on_device(): from_low = lax.ppermute(to_high, 'dev', forward)  5.41 us
    ppermute x3, starting transfers between devices, ring(): lax.ppermute(array, 'grp', [(i, (i + shift) % count) for i in range(count)])  3.66 us
    ppermute x1, waiting for transfers between devices, on_device(): from_high = lax.ppermute(to_low, 'dev', backward)  3.12 us
    pallas_call x1, Pallas kernels, on_device(): pl.pallas_call(functools.partial(pack_kernel, capacity=capacity, wide=wid...  2.01 us
    ppermute x1, starting transfers between devices, on_device(): from_high = lax.ppermute(to_low, 'dev', backward)  1.92 us
    ppermute x3, waiting for transfers between devices, ring(): lax.ppermute(array, 'grp', [(i, (i + shift) % count) for i in range(count)])  1.22 us
  transfers between devices with their start and end apart: 5, of which 2 were waited for; matrix products, arithmetic and copies ran while one was open for 0% of the time, Pallas kernels for 0%

profile of v3, /device:TPU:1, one launch (start us, length us, event | category | flops | bytes accessed | tf_op | source)
XLA Modules:
  0.0 37.7 jit_solution(10558561540984977989)
XLA Ops:
  0.6 2.0 %pack.1 = f32[8,24,256]{2,1,0:T(8,128)S(1)} custom-call(f32[3,4096]{1,0:T(4,128)} %coord.1, f32[1,4096]{1,0:T(1,128)} %bitcast.9, f32[1,4096]{1,0:T(1,128)} %bitcast.10, s32[1,4096]{1,0:T(1,128)} %bitcast.11, s32[1,4096]{1,0:T(1,128)} %bitcast.12, s32[1,4096]{1,0:T(1,128)} %bitcast.13), custom_call_target="tpu_custom_call" | custom-call | tf_op jit(solution)/shard_map/pack/pallas_call | solution.py:266
  2.6 12.7 %all_to_all.5.got = f32[8,24,256]{2,1,0:T(8,128)S(1)} all-to-all(f32[8,24,256]{2,1,0:T(8,128)S(1)} %pack.1), channel_id=1, replica_groups=mesh['grp'=4,'dev'=8] {'dev'}, dimensions={0} | all-to-all | bytes 393216 | tf_op jit(solution)/shard_map/all_to_all | solution.py:272
  15.3 5.5 %field.1 = (f32[256,512]{1,0:T(8,128)S(1)}, f32[40,128]{1,0:T(8,128)S(1)}, f32[40,128]{1,0:T(8,128)S(1)}, f32[8,128]{1,0:T(8,128)S(1)}) custom-call(f32[8,24,256]{2,1,0:T(8,128)S(1)} %all_to_all.5.got), custom_call_target="tpu_custom_call" | custom-call | tf_op jit(solution)/shard_map/field/pallas_call | solution.py:274
  20.8 1.3 %collective-permute-start = (f32[40,128]{1,0:T(8,128)S(1)}, f32[40,128]{1,0:T(8,128)S(1)}, u32[]{:S(2)}, u32[]{:S(2)}) collective-permute-start(f32[40,128]{1,0:T(8,128)S(1)} %get-tuple-element.10), channel_id=1, source_target_pairs={{0,8},{8,16},{16,24},{24,0},{1,9},{9,17},{17,25},{25,1},{2,10},{10... | collective-permute-start | bytes 61448 | tf_op jit(solution)/shard_map/ppermute | solution.py:251
  22.1 1.2 %collective-permute-start.1 = (f32[40,128]{1,0:T(8,128)S(1)}, f32[40,128]{1,0:T(8,128)S(1)}, u32[]{:S(2)}, u32[]{:S(2)}) collective-permute-start(f32[40,128]{1,0:T(8,128)S(1)} %get-tuple-element.11), channel_id=1, source_target_pairs={{0,24},{8,0},{16,8},{24,16},{1,25},{9,1},{17,9},{25,17},{2,26},{10... | collective-permute-start | bytes 61448 | tf_op jit(solution)/shard_map/ppermute | solution.py:251
  23.2 1.2 %collective-permute-start.2 = (f32[8,128]{1,0:T(8,128)S(1)}, f32[8,128]{1,0:T(8,128)S(1)}, u32[]{:S(2)}, u32[]{:S(2)}) collective-permute-start(f32[8,128]{1,0:T(8,128)S(1)} %get-tuple-element.12.rest_0_), channel_id=1, source_target_pairs={{0,16},{8,24},{16,0},{24,8},{1,17},{9,25},{17,1},{25,9},{2,18},{10... | collective-permute-start | bytes 12296 | tf_op jit(solution)/shard_map/ppermute | solution.py:251
  24.5 1.2 %collective-permute-done.2.rest_1_ = f32[8,128]{1,0:T(8,128)S(1)} collective-permute-done((f32[8,128]{1,0:T(8,128)S(1)}, f32[8,128]{1,0:T(8,128)S(1)}, u32[]{:S(2)}, u32[]{:S(2)}) %collective-permute-start.2) | collective-permute-done | bytes 4128 | tf_op jit(solution)/shard_map/ppermute | solution.py:251
  25.7 0.0 collective-permute-done.from_below
  25.7 0.0 collective-permute-done.1.from_above
  25.7 0.6 %edge.1 = (f32[32,128]{1,0:T(8,128)S(1)}, f32[32,128]{1,0:T(8,128)S(1)}, f32[1,128]{1,0:T(1,128)}) custom-call(f32[256,512]{1,0:T(8,128)S(1)} %get-tuple-element.9.field, f32[40,128]{1,0:T(8,128)S(1)} %collective-permute-done.from_below, f32[40,128]{1,0:T(8,128)S(1)} %collective-permute-done.1.from_above, f32[8,128]{1,0:T(8,128)S(1)} %get-tuple-element.12.rest_0_, ...), custom_call_target="tpu_custom_call" | custom-call | tf_op jit(solution)/shard_map/edge/pallas_call | solution.py:297
  26.3 5.4 %collective-permute-start.3 = (f32[32,128]{1,0:T(8,128)S(1)}, f32[32,128]{1,0:T(8,128)S(1)}, u32[]{:S(2)}, u32[]{:S(2)}) collective-permute-start(f32[32,128]{1,0:T(8,128)S(1)} %get-tuple-element.13), channel_id=1, source_target_pairs={{0,1},{1,2},{2,3},{3,4},{4,5},{5,6},{6,7},{8,9},{9,10},{10,11},{11... | collective-permute-start | bytes 49160 | tf_op jit(solution)/shard_map/ppermute | solution.py:304
  31.7 1.9 %collective-permute-start.4 = (f32[32,128]{1,0:T(8,128)S(1)}, f32[32,128]{1,0:T(8,128)S(1)}, u32[]{:S(2)}, u32[]{:S(2)}) collective-permute-start(f32[32,128]{1,0:T(8,128)S(1)} %get-tuple-element.14), channel_id=1, source_target_pairs={{1,0},{2,1},{3,2},{4,3},{5,4},{6,5},{7,6},{9,8},{10,9},{11,10},{12... | collective-permute-start | bytes 49160 | tf_op jit(solution)/shard_map/ppermute | solution.py:305
  33.6 0.0 collective-permute-done.3.from_low
  33.6 3.1 %collective-permute-done.4.from_high = f32[32,128]{1,0:T(8,128)S(1)} collective-permute-done((f32[32,128]{1,0:T(8,128)S(1)}, f32[32,128]{1,0:T(8,128)S(1)}, u32[]{:S(2)}, u32[]{:S(2)}) %collective-permute-start.4) | collective-permute-done | bytes 16416 | tf_op jit(solution)/shard_map/ppermute | solution.py:305
  36.8 0.9 %finish.1 = f32[256,512]{1,0:T(8,128)} custom-call(f32[256,512]{1,0:T(8,128)S(1)} %get-tuple-element.9.field, f32[40,128]{1,0:T(8,128)S(1)} %collective-permute-done.from_below, f32[40,128]{1,0:T(8,128)S(1)} %collective-permute-done.1.from_above, f32[32,128]{1,0:T(8,128)S(1)} %collective-permute-done.3.from_low, f32[32,128]{1,0:T(8,128)S(1)} %collective-permute-done.4.from_high), custom_call_target="tpu_custom_call" | custom-call | tf_op jit(solution)/shard_map/finish/pallas_call | solution.py:306
Async XLA Ops:
  20.8 4.9 %collective-permute-start = (f32[40,128]{1,0:T(8,128)S(1)}, f32[40,128]{1,0:T(8,128)S(1)}, u32[]{:S(2)}, u32[]{:S(2)}) collective-permute-start(f32[40,128]{1,0:T(8,128)S(1)} %get-tuple-element.10), channel_id=1, source_target_pairs={{0,8},{8,16},{16,24},{24,0},{1,9},{9,17},{17,25},{25,1},{2,10},{10... | collective-permute-start | bytes 61448 | tf_op jit(solution)/shard_map/ppermute | solution.py:251
  22.1 3.6 %collective-permute-start.1 = (f32[40,128]{1,0:T(8,128)S(1)}, f32[40,128]{1,0:T(8,128)S(1)}, u32[]{:S(2)}, u32[]{:S(2)}) collective-permute-start(f32[40,128]{1,0:T(8,128)S(1)} %get-tuple-element.11), channel_id=1, source_target_pairs={{0,24},{8,0},{16,8},{24,16},{1,25},{9,1},{17,9},{25,17},{2,26},{10... | collective-permute-start | bytes 61448 | tf_op jit(solution)/shard_map/ppermute | solution.py:251
  23.2 2.5 %collective-permute-start.2 = (f32[8,128]{1,0:T(8,128)S(1)}, f32[8,128]{1,0:T(8,128)S(1)}, u32[]{:S(2)}, u32[]{:S(2)}) collective-permute-start(f32[8,128]{1,0:T(8,128)S(1)} %get-tuple-element.12.rest_0_), channel_id=1, source_target_pairs={{0,16},{8,24},{16,0},{24,8},{1,17},{9,25},{17,1},{25,9},{2,18},{10... | collective-permute-start | bytes 12296 | tf_op jit(solution)/shard_map/ppermute | solution.py:251
  26.3 7.4 %collective-permute-start.3 = (f32[32,128]{1,0:T(8,128)S(1)}, f32[32,128]{1,0:T(8,128)S(1)}, u32[]{:S(2)}, u32[]{:S(2)}) collective-permute-start(f32[32,128]{1,0:T(8,128)S(1)} %get-tuple-element.13), channel_id=1, source_target_pairs={{0,1},{1,2},{2,3},{3,4},{4,5},{5,6},{6,7},{8,9},{9,10},{10,11},{11... | collective-permute-start | bytes 49160 | tf_op jit(solution)/shard_map/ppermute | solution.py:304
  31.7 5.1 %collective-permute-start.4 = (f32[32,128]{1,0:T(8,128)S(1)}, f32[32,128]{1,0:T(8,128)S(1)}, u32[]{:S(2)}, u32[]{:S(2)}) collective-permute-start(f32[32,128]{1,0:T(8,128)S(1)} %get-tuple-element.14), channel_id=1, source_target_pairs={{1,0},{2,1},{3,2},{4,3},{5,4},{6,5},{7,6},{9,8},{10,9},{11,10},{12... | collective-permute-start | bytes 49160 | tf_op jit(solution)/shard_map/ppermute | solution.py:305

commit v4 on v3

--- a/solution.py
+++ b/solution.py
@@ -92,6 +92,8 @@
     for i in range(NODES):
         scale = jnp.where(node == i, SCALES[i], scale)
     elem_ids = lax.broadcasted_iota(jnp.int32, (ELEM_DEV, wide), 0).astype(jnp.float32)
+    elem_ids = elem_ids.astype(jnp.bfloat16)
+    one = jnp.ones((ELEM_DEV, wide), jnp.bfloat16)
     acc[...] = jnp.zeros_like(acc)
 
     def step(i, carry):
@@ -102,7 +104,7 @@
                 got[peer, row + k * per_peer : row + k * per_peer + 1, :] for k in range(FIELDS)
             )
             lanes = slice(q * wide, (q + 1) * wide)
-            elems[:, lanes] = jnp.where(elem_ids == e, 1.0, 0.0).astype(jnp.bfloat16)
+            elems[:, lanes] = jnp.where(elem_ids == e.astype(jnp.bfloat16), one, jnp.zeros_like(one))
             first_w = basis_of(u, node, scale) * f
             second_w = basis_of(v, node, scale)
             third_w = basis_of(w, node, scale)

time: 37.9 us -> 37.9 us (level)
  no operation moved by 1% of the time
where the time goes in v4:
time: 37.9 us; the launch traced here: 37.7 us
  blocking collectives  12.7 us (34%)
  starting transfers between devices  11 us (29%)
  Pallas kernels  8.97 us (24%)
  waiting for transfers between devices  4.35 us (11%)
  between operations  0.67 us (2%)
    all_to_all x1, blocking collectives, on_device(): got = lax.all_to_all(send, 'dev', split_axis=0, concat_axis=0, tiled=True)  12.7 us
    pallas_call x1, Pallas kernels, on_device(): pl.pallas_call(functools.partial(field_kernel, capacity=capacity, wide=wi...  5.47 us
    ppermute x1, starting transfers between devices, on_device(): from_low = lax.ppermute(to_high, 'dev', forward)  5.41 us
    ppermute x3, starting transfers between devices, ring(): lax.ppermute(array, 'grp', [(i, (i + shift) % count) for i in range(count)])  3.66 us
    ppermute x1, waiting for transfers between devices, on_device(): from_high = lax.ppermute(to_low, 'dev', backward)  3.12 us
    pallas_call x1, Pallas kernels, on_device(): pl.pallas_call(functools.partial(pack_kernel, capacity=capacity, wide=wid...  2.01 us
    ppermute x1, starting transfers between devices, on_device(): from_high = lax.ppermute(to_low, 'dev', backward)  1.92 us
    ppermute x3, waiting for transfers between devices, ring(): lax.ppermute(array, 'grp', [(i, (i + shift) % count) for i in range(count)])  1.22 us
  transfers between devices with their start and end apart: 5, of which 2 were waited for; matrix products, arithmetic and copies ran while one was open for 0% of the time, Pallas kernels for 0%

profile of v4, /device:TPU:1, one launch (start us, length us, event | category | flops | bytes accessed | tf_op | source)
XLA Modules:
  0.0 37.7 jit_solution(13577433112151096517)
XLA Ops:
  0.6 2.0 %pack.1 = f32[8,24,256]{2,1,0:T(8,128)S(1)} custom-call(f32[3,4096]{1,0:T(4,128)} %coord.1, f32[1,4096]{1,0:T(1,128)} %bitcast.9, f32[1,4096]{1,0:T(1,128)} %bitcast.10, s32[1,4096]{1,0:T(1,128)} %bitcast.11, s32[1,4096]{1,0:T(1,128)} %bitcast.12, s32[1,4096]{1,0:T(1,128)} %bitcast.13), custom_call_target="tpu_custom_call" | custom-call | tf_op jit(solution)/shard_map/pack/pallas_call | solution.py:268
  2.6 12.7 %all_to_all.5.got = f32[8,24,256]{2,1,0:T(8,128)S(1)} all-to-all(f32[8,24,256]{2,1,0:T(8,128)S(1)} %pack.1), channel_id=1, replica_groups=mesh['grp'=4,'dev'=8] {'dev'}, dimensions={0} | all-to-all | bytes 393216 | tf_op jit(solution)/shard_map/all_to_all | solution.py:274
  15.3 5.5 %field.1 = (f32[256,512]{1,0:T(8,128)S(1)}, f32[40,128]{1,0:T(8,128)S(1)}, f32[40,128]{1,0:T(8,128)S(1)}, f32[8,128]{1,0:T(8,128)S(1)}) custom-call(f32[8,24,256]{2,1,0:T(8,128)S(1)} %all_to_all.5.got), custom_call_target="tpu_custom_call" | custom-call | tf_op jit(solution)/shard_map/field/pallas_call | solution.py:276
  20.8 1.3 %collective-permute-start = (f32[40,128]{1,0:T(8,128)S(1)}, f32[40,128]{1,0:T(8,128)S(1)}, u32[]{:S(2)}, u32[]{:S(2)}) collective-permute-start(f32[40,128]{1,0:T(8,128)S(1)} %get-tuple-element.10), channel_id=1, source_target_pairs={{0,8},{8,16},{16,24},{24,0},{1,9},{9,17},{17,25},{25,1},{2,10},{10... | collective-permute-start | bytes 61448 | tf_op jit(solution)/shard_map/ppermute | solution.py:253
  22.1 1.2 %collective-permute-start.1 = (f32[40,128]{1,0:T(8,128)S(1)}, f32[40,128]{1,0:T(8,128)S(1)}, u32[]{:S(2)}, u32[]{:S(2)}) collective-permute-start(f32[40,128]{1,0:T(8,128)S(1)} %get-tuple-element.11), channel_id=1, source_target_pairs={{0,24},{8,0},{16,8},{24,16},{1,25},{9,1},{17,9},{25,17},{2,26},{10... | collective-permute-start | bytes 61448 | tf_op jit(solution)/shard_map/ppermute | solution.py:253
  23.2 1.2 %collective-permute-start.2 = (f32[8,128]{1,0:T(8,128)S(1)}, f32[8,128]{1,0:T(8,128)S(1)}, u32[]{:S(2)}, u32[]{:S(2)}) collective-permute-start(f32[8,128]{1,0:T(8,128)S(1)} %get-tuple-element.12.rest_0_), channel_id=1, source_target_pairs={{0,16},{8,24},{16,0},{24,8},{1,17},{9,25},{17,1},{25,9},{2,18},{10... | collective-permute-start | bytes 12296 | tf_op jit(solution)/shard_map/ppermute | solution.py:253
  24.5 1.2 %collective-permute-done.2.rest_1_ = f32[8,128]{1,0:T(8,128)S(1)} collective-permute-done((f32[8,128]{1,0:T(8,128)S(1)}, f32[8,128]{1,0:T(8,128)S(1)}, u32[]{:S(2)}, u32[]{:S(2)}) %collective-permute-start.2) | collective-permute-done | bytes 4128 | tf_op jit(solution)/shard_map/ppermute | solution.py:253
  25.7 0.0 collective-permute-done.from_below
  25.7 0.0 collective-permute-done.1.from_above
  25.7 0.6 %edge.1 = (f32[32,128]{1,0:T(8,128)S(1)}, f32[32,128]{1,0:T(8,128)S(1)}, f32[1,128]{1,0:T(1,128)}) custom-call(f32[256,512]{1,0:T(8,128)S(1)} %get-tuple-element.9.field, f32[40,128]{1,0:T(8,128)S(1)} %collective-permute-done.from_below, f32[40,128]{1,0:T(8,128)S(1)} %collective-permute-done.1.from_above, f32[8,128]{1,0:T(8,128)S(1)} %get-tuple-element.12.rest_0_, ...), custom_call_target="tpu_custom_call" | custom-call | tf_op jit(solution)/shard_map/edge/pallas_call | solution.py:299
  26.3 5.4 %collective-permute-start.3 = (f32[32,128]{1,0:T(8,128)S(1)}, f32[32,128]{1,0:T(8,128)S(1)}, u32[]{:S(2)}, u32[]{:S(2)}) collective-permute-start(f32[32,128]{1,0:T(8,128)S(1)} %get-tuple-element.13), channel_id=1, source_target_pairs={{0,1},{1,2},{2,3},{3,4},{4,5},{5,6},{6,7},{8,9},{9,10},{10,11},{11... | collective-permute-start | bytes 49160 | tf_op jit(solution)/shard_map/ppermute | solution.py:306
  31.7 1.9 %collective-permute-start.4 = (f32[32,128]{1,0:T(8,128)S(1)}, f32[32,128]{1,0:T(8,128)S(1)}, u32[]{:S(2)}, u32[]{:S(2)}) collective-permute-start(f32[32,128]{1,0:T(8,128)S(1)} %get-tuple-element.14), channel_id=1, source_target_pairs={{1,0},{2,1},{3,2},{4,3},{5,4},{6,5},{7,6},{9,8},{10,9},{11,10},{12... | collective-permute-start | bytes 49160 | tf_op jit(solution)/shard_map/ppermute | solution.py:307
  33.6 0.0 collective-permute-done.3.from_low
  33.6 3.1 %collective-permute-done.4.from_high = f32[32,128]{1,0:T(8,128)S(1)} collective-permute-done((f32[32,128]{1,0:T(8,128)S(1)}, f32[32,128]{1,0:T(8,128)S(1)}, u32[]{:S(2)}, u32[]{:S(2)}) %collective-permute-start.4) | collective-permute-done | bytes 16416 | tf_op jit(solution)/shard_map/ppermute | solution.py:307
  36.8 0.9 %finish.1 = f32[256,512]{1,0:T(8,128)} custom-call(f32[256,512]{1,0:T(8,128)S(1)} %get-tuple-element.9.field, f32[40,128]{1,0:T(8,128)S(1)} %collective-permute-done.from_below, f32[40,128]{1,0:T(8,128)S(1)} %collective-permute-done.1.from_above, f32[32,128]{1,0:T(8,128)S(1)} %collective-permute-done.3.from_low, f32[32,128]{1,0:T(8,128)S(1)} %collective-permute-done.4.from_high), custom_call_target="tpu_custom_call" | custom-call | tf_op jit(solution)/shard_map/finish/pallas_call | solution.py:308
Async XLA Ops:
  20.8 4.9 %collective-permute-start = (f32[40,128]{1,0:T(8,128)S(1)}, f32[40,128]{1,0:T(8,128)S(1)}, u32[]{:S(2)}, u32[]{:S(2)}) collective-permute-start(f32[40,128]{1,0:T(8,128)S(1)} %get-tuple-element.10), channel_id=1, source_target_pairs={{0,8},{8,16},{16,24},{24,0},{1,9},{9,17},{17,25},{25,1},{2,10},{10... | collective-permute-start | bytes 61448 | tf_op jit(solution)/shard_map/ppermute | solution.py:253
  22.1 3.6 %collective-permute-start.1 = (f32[40,128]{1,0:T(8,128)S(1)}, f32[40,128]{1,0:T(8,128)S(1)}, u32[]{:S(2)}, u32[]{:S(2)}) collective-permute-start(f32[40,128]{1,0:T(8,128)S(1)} %get-tuple-element.11), channel_id=1, source_target_pairs={{0,24},{8,0},{16,8},{24,16},{1,25},{9,1},{17,9},{25,17},{2,26},{10... | collective-permute-start | bytes 61448 | tf_op jit(solution)/shard_map/ppermute | solution.py:253
  23.2 2.5 %collective-permute-start.2 = (f32[8,128]{1,0:T(8,128)S(1)}, f32[8,128]{1,0:T(8,128)S(1)}, u32[]{:S(2)}, u32[]{:S(2)}) collective-permute-start(f32[8,128]{1,0:T(8,128)S(1)} %get-tuple-element.12.rest_0_), channel_id=1, source_target_pairs={{0,16},{8,24},{16,0},{24,8},{1,17},{9,25},{17,1},{25,9},{2,18},{10... | collective-permute-start | bytes 12296 | tf_op jit(solution)/shard_map/ppermute | solution.py:253
  26.3 7.3 %collective-permute-start.3 = (f32[32,128]{1,0:T(8,128)S(1)}, f32[32,128]{1,0:T(8,128)S(1)}, u32[]{:S(2)}, u32[]{:S(2)}) collective-permute-start(f32[32,128]{1,0:T(8,128)S(1)} %get-tuple-element.13), channel_id=1, source_target_pairs={{0,1},{1,2},{2,3},{3,4},{4,5},{5,6},{6,7},{8,9},{9,10},{10,11},{11... | collective-permute-start | bytes 49160 | tf_op jit(solution)/shard_map/ppermute | solution.py:306
  31.7 5.1 %collective-permute-start.4 = (f32[32,128]{1,0:T(8,128)S(1)}, f32[32,128]{1,0:T(8,128)S(1)}, u32[]{:S(2)}, u32[]{:S(2)}) collective-permute-start(f32[32,128]{1,0:T(8,128)S(1)} %get-tuple-element.14), channel_id=1, source_target_pairs={{1,0},{2,1},{3,2},{4,3},{5,4},{6,5},{7,6},{9,8},{10,9},{11,10},{12... | collective-permute-start | bytes 49160 | tf_op jit(solution)/shard_map/ppermute | solution.py:307
